TPU v7x, 32 devices: a whole 2x2x4 slice. The times are simulated.
32 devices in a mesh: ep: 8 (over z, y), tp: 4 (over x, core).
Axes of the slice: x: 2, y: 2, z: 4, core: 2. Of those that a mesh axis runs over, the one named last changes fastest.
Arguments:
- tokens: bfloat16 [1024, 4096], P('ep'), may hold values from -6 to 6
- expert_ids: int32 [1024, 2], P('ep'), may hold values from 0 to 7, all different within a row; in each aligned block of 128 rows (0 to 127, 128 to 255, ...) at most 64 rows name the same one
- gate_logits: float32 [1024, 2], P('ep'), may hold values from -6 to 6
- w_gate: bfloat16 [8, 4096, 14336], P('ep', None, 'tp'), may hold values from -0.09375 to 0.09375
- w_up: bfloat16 [8, 4096, 14336], P('ep', None, 'tp'), may hold values from -0.09375 to 0.09375
- w_down: bfloat16 [8, 14336, 4096], P('ep', 'tp'), may hold values from -0.046875 to 0.046875
Outputs:
- output: bfloat16 [1024, 4096], P('ep', 'tp')
Inputs may be any that keep to these rules, and one draw needn't show every extreme that they name: `expert_ids`: the 2 ids of a token differ. Among the 128 rows of one index of ep no expert is named more than 64 times, a bound that some block reaches.
All inputs are finite; a program needn't handle non-finite values.
Results may differ from a plain program's by a relative error of at most 0.014.
Values may be sent and summed in bfloat16 or wider, within the bound.
A program may use at most 192 MiB of HBM per device.

v0:
```python
import jax
import jax.numpy as jnp
from jax import lax
from jax.sharding import PartitionSpec as P

EXPERTS = 8
TOP = 2


def shards(tokens, expert_ids, gate_logits, w_gate, w_up, w_down):
    tok_count = tokens.shape[0]
    width = tokens.shape[1]
    ep_count = lax.axis_size("ep")
    tp_count = lax.axis_size("tp")
    group = ep_count // EXPERTS
    capacity = tok_count // 2
    first = 1.0 / (1.0 + jnp.exp(gate_logits[:, 1] - gate_logits[:, 0]))
    second = 1.0 / (1.0 + jnp.exp(gate_logits[:, 0] - gate_logits[:, 1]))
    gate_flat = jnp.stack([first, second], axis=1).reshape(-1)
    flat_ids = expert_ids.reshape(-1)
    onehot = (flat_ids[:, None] == jnp.arange(EXPERTS, dtype=jnp.int32)[None, :]).astype(jnp.int32)
    slot = jnp.sum((jnp.cumsum(onehot, axis=0) - onehot) * onehot, axis=1)
    assigned = flat_ids.shape[0]
    owner = jnp.arange(assigned, dtype=jnp.int32) // TOP
    table = (
        jnp.full((EXPERTS * capacity,), tok_count, jnp.int32)
        .at[flat_ids * capacity + slot]
        .set(owner)
    )
    share = width // tp_count
    source_rows = lax.dynamic_slice_in_dim(tokens, lax.axis_index("tp") * share, share, 1)
    padded = jnp.concatenate(
        [source_rows, jnp.zeros((1, source_rows.shape[1]), tokens.dtype)], axis=0
    )
    packed = padded[table].reshape(EXPERTS, capacity, source_rows.shape[1])
    outgoing = jnp.repeat(packed, group, axis=0)
    offsets = jnp.arange(group, dtype=jnp.int32)
    columns = (flat_ids[:, None] * group + offsets[None, :]) * capacity + slot[:, None]
    received = lax.all_to_all(outgoing, "ep", split_axis=0, concat_axis=0, tiled=True)
    received = lax.all_gather(received, "tp", axis=2, tiled=True)
    slots = received.shape[1]
    rows = received.reshape(-1, width)
    gate = jnp.dot(rows, w_gate[0], preferred_element_type=jnp.float32)
    upper = jnp.dot(rows, w_up[0], preferred_element_type=jnp.float32)
    hidden = (jax.nn.silu(gate) * upper).astype(jnp.bfloat16)
    wpiece = w_down[0]
    shares = lax.psum_scatter(
        lax.dot_general(
            wpiece, hidden, (((0,), (1,)), ((), ())), preferred_element_type=jnp.float32
        ).astype(jnp.bfloat16),
        "tp",
        scatter_dimension=0,
        tiled=True,
    ).astype(jnp.float32)
    shares = shares.reshape(width // tp_count, ep_count, slots)
    returned = lax.all_to_all(
        shares.astype(jnp.bfloat16), "ep", split_axis=1, concat_axis=1, tiled=True
    ).astype(shares.dtype)
    results = returned.reshape(width // tp_count, ep_count * capacity)
    picked = jnp.take(results, columns.reshape(-1), axis=1).reshape(
        width // tp_count, assigned, group
    )
    summed = jnp.sum(picked, axis=2) * gate_flat[None, :]
    combined = jnp.sum(summed.reshape(width // tp_count, tok_count, TOP), axis=2)
    return jnp.transpose(combined).astype(jnp.bfloat16)


def solution(mesh):
    placed = (
        P("ep", None),
        P("ep", None),
        P("ep", None),
        P("ep", None, "tp"),
        P("ep", None, "tp"),
        P("ep", "tp", None),
    )
    return jax.shard_map(
        shards, mesh=mesh, in_specs=placed, out_specs=P("ep", "tp"), check_vma=False
    )
```

profile of v0, /device:TPU:28, one launch (start us, length us, event | category | flops | bytes accessed | tf_op | source)
XLA Modules:
  0.0 238.0 jit_solution(6963268963990315639)
XLA Ops:
  6.5 0.0 copy-start
  6.5 0.0 all-gather.2.cloned.1.call-start
  6.5 0.9 copy.13
  7.4 0.1 eq.26
  7.6 0.1 broadcast_in_dim_reshape.2
  7.7 0.7 broadcast_multiply_fusion
  8.4 0.6 reduce-window.6
  9.0 0.2 slice_reduce_fusion
  9.2 0.1 copy.17
  9.3 0.1 mul.51
  9.5 0.1 fusion.22
  9.6 1.4 scatter_custom_fusion
  11.0 0.0 copy-done
  11.1 2.1 gather_fusion
  13.2 29.3 %all_to_all.10 = bf16[8,64,1024]{2,1,0:T(8,128)(2,1)} all-to-all(bf16[8,64,1024]{2,1,0:T(8,128)(2,1)S(1)} %bitcast.56), channel_id=1, replica_groups=mesh['ep'=8,'tp'=4] {'ep'}, dimensions={0} | all-to-all | bytes 2097152 | tf_op jit(solution)/shard_map/all_to_all | solution.py:39
  42.4 0.0 all-gather.2.cloned.1.call-update
  42.4 0.2 reduce-scatter.2.cloned.1.call-start
  42.7 35.3 %all-gather.2.cloned.1.call-done = bf16[8,64,4096]{2,1,0:T(8,128)(2,1)} async-done(((bf16[8,64,1024]{2,1,0:T(8,128)(2,1)}), bf16[8,64,4096]{2,1,0:T(8,128)(2,1)}) %all-gather.2.cloned.1.call-update) | async-done | bytes 4194320 | tf_op jit(solution)/shard_map/all_gather | solution.py:40
  78.0 23.7 %fusion.4 = f32[512,3584]{1,0:T(8,128)} fusion(bf16[512,4096]{1,0:T(8,128)(2,1)} %bitcast.62, bf16[1,4096,3584]{2,1,0:T(8,128)(2,1)} %param.9), kind=kOutput, calls=%fused_computation.7 | convolution fusion | flops 15032385536 | bytes 40894464 | tf_op jit(solution)/shard_map/dot_general | solution.py:43
  101.7 24.7 %multiply_convert_fusion.clone.8 = bf16[512,3584]{1,0:T(8,128)(2,1)} fusion(f32[512,3584]{1,0:T(8,128)} %fusion.4, bf16[512,4096]{1,0:T(8,128)(2,1)} %bitcast.63, bf16[1,4096,3584]{2,1,0:T(8,128)(2,1)} %param.10), kind=kOutput, calls=%fused_computation.9.clone.clone.clone.clone.clone.clone.clone.1 | convolution fusion | flops 15043395584 | bytes 44564480 | tf_op jit(solution)/shard_map/dot_general | solution.py:44
  126.3 0.0 copy-start.2
  126.4 0.0 copy-start.3
  126.4 23.3 %fusion.15 = bf16[4096,512]{0,1:T(8,128)(2,1)} fusion(bf16[1,3584,4096]{2,1,0:T(8,128)(2,1)} %param.11, bf16[512,3584]{1,0:T(8,128)(2,1)} %multiply_convert_fusion.clone.8), kind=kOutput, calls=%fused_computation.11 | convolution fusion | flops 15034482688 | bytes 37224448 | tf_op jit(solution)/shard_map/dot_general | solution.py:48
  149.6 0.0 reduce-scatter.2.cloned.1.call-update
  149.7 44.6 %reduce-scatter.2.cloned.1.call-done = bf16[1024,512]{0,1:T(8,128)(2,1)} async-done(((bf16[4096,512]{0,1:T(8,128)(2,1)}), bf16[1024,512]{0,1:T(8,128)(2,1)}) %reduce-scatter.2.cloned.1.call-update) | async-done | bytes 1048592 | tf_op jit(solution)/shard_map/reduce_scatter | solution.py:47
  194.2 6.0 %all-to-all-start.1 = ((bf16[1024,8,64]{0,2,1:T(8,128)(2,1)}), bf16[1024,8,64]{0,2,1:T(8,128)(2,1)}, u32[]{:S(2)}, u32[]{:S(2)}) async-start(bf16[1024,8,64]{0,2,1:T(8,128)(2,1)} %bitcast.58), calls=%async_computation.2 | async-start | bytes 2097152 | tf_op jit(solution)/shard_map/all_to_all | solution.py:56
  200.2 0.1 reduce_sum.27
  200.3 0.1 copy.15
  200.4 0.0 copy-done.2
  200.4 0.1 copy.16
  200.6 0.0 copy-done.3
  200.6 0.1 copy.18
  200.7 0.0 copy-start.1
  200.8 22.8 %all-to-all-done.1 = bf16[1024,8,64]{0,2,1:T(8,128)(2,1)} async-done(((bf16[1024,8,64]{0,2,1:T(8,128)(2,1)}), bf16[1024,8,64]{0,2,1:T(8,128)(2,1)}, u32[]{:S(2)}, u32[]{:S(2)}) %all-to-all-start.1) | async-done | bytes 1048608 | tf_op jit(solution)/shard_map/all_to_all | solution.py:56
  223.5 1.5 bitcast_convert_fusion
  225.0 2.0 gather_fusion.1
  227.0 1.8 gather.11
  228.9 2.3 multiply_reduce_fusion
  231.1 0.0 copy-done.1
  (13 shorter events, 0.2 us)
Async XLA Ops:
  6.5 4.5 %copy-start = (bf16[128,4096]{1,0:T(8,128)(2,1)S(1)}, bf16[128,4096]{1,0:T(8,128)(2,1)}, u32[]{:S(2)}) copy-start(bf16[128,4096]{1,0:T(8,128)(2,1)} %param.6) | copy-start | bytes 3145732
  6.5 71.4 %all-gather.2.cloned.1.call-start = ((), (), s32[]{:S(2)}) async-start(), calls=%async_computation.3 | async-start | bytes 5242880 | tf_op jit(solution)/shard_map/all_gather | solution.py:40
  42.4 151.8 %reduce-scatter.2.cloned.1.call-start = ((), (), s32[]{:S(2)}) async-start(), calls=%async_computation.4 | async-start | bytes 5242880 | tf_op jit(solution)/shard_map/reduce_scatter | solution.py:47
  126.3 74.1 %copy-start.2 = (s32[128,2]{0,1:T(2,128)S(1)}, s32[128,2]{0,1:T(2,128)}, u32[]{:S(2)}) copy-start(s32[128,2]{0,1:T(2,128)} %param.7) | copy-start | bytes 3076
  126.4 74.2 %copy-start.3 = (f32[128,2]{0,1:T(2,128)S(1)}, f32[128,2]{0,1:T(2,128)}, u32[]{:S(2)}) copy-start(f32[128,2]{0,1:T(2,128)} %param.8) | copy-start | bytes 3076
  194.2 29.3 %all-to-all-start.1 = ((bf16[1024,8,64]{0,2,1:T(8,128)(2,1)}), bf16[1024,8,64]{0,2,1:T(8,128)(2,1)}, u32[]{:S(2)}, u32[]{:S(2)}) async-start(bf16[1024,8,64]{0,2,1:T(8,128)(2,1)} %bitcast.58), calls=%async_computation.2 | async-start | bytes 2097152 | tf_op jit(solution)/shard_map/all_to_all | solution.py:56
  200.7 30.4 %copy-start.1 = (bf16[128,4096]{1,0:T(8,128)(2,1)S(1)}, bf16[128,4096]{1,0:T(8,128)(2,1)}, u32[]{:S(2)}) copy-start(bf16[128,4096]{1,0:T(8,128)(2,1)} %param.6) | copy-start | bytes 3145732
Sparse Core Ops, SparseCore 0:
  42.6 35.3 all-gather.1
  149.8 44.3 reduce-scatter.1
where the time goes:
time: 242 us; the launch traced here: 238 us
  waiting for transfers between devices  103 us (43%)
  matrix products  71.6 us (30%)
  blocking collectives  29.3 us (12%)
  between operations  13.5 us (6%)
  local copies, waits for them, and re-layouts  9.46 us (4%)
  starting transfers between devices  6.22 us (3%)
  other arithmetic  5.2 us (2%)
    reduce_scatter x1, waiting for transfers between devices, shards(): lax.psum_scatter(lax.dot_general(wpiece, hidden, (((0,), (1,)), ((), ()))...  44.6 us
    all_gather x1, waiting for transfers between devices, shards(): received = lax.all_gather(received, 'tp', axis=2, tiled=True)  35.3 us
    all_to_all x1, blocking collectives, shards(): lax.all_to_all(outgoing, 'ep', split_axis=0, concat_axis=0, tiled=True)  29.3 us
    dot_general x1, matrix products, shards(): upper = jnp.dot(rows, w_up[0], preferred_element_type=jnp.float32)  24.7 us
    dot_general x1, matrix products, shards(): gate = jnp.dot(rows, w_gate[0], preferred_element_type=jnp.float32)  23.7 us
    dot_general x1, matrix products, shards(): lax.dot_general(wpiece, hidden, (((0,), (1,)), ((), ())), preferred_eleme...  23.3 us
    all_to_all x1, waiting for transfers between devices, shards(): lax.all_to_all(shares.astype(jnp.bfloat16), 'ep', split_axis=1, concat_ax...  22.8 us
    all_to_all x1, starting transfers between devices, shards(): lax.all_to_all(shares.astype(jnp.bfloat16), 'ep', split_axis=1, concat_ax...  6 us
  transfers between devices with their start and end apart: 3, of which 3 were waited for; matrix products, arithmetic and copies ran while one was open for 0% of the time, Pallas kernels for 0%

commit v1 on v0

v1 whole, which is shorter than its diff:
```python
import functools

import jax
import jax.numpy as jnp
from jax import lax
from jax.experimental import pallas as pl
from jax.experimental.pallas import tpu as pltpu
from jax.sharding import PartitionSpec as P

EXPERTS = 8
TOP = 2
CORES = 2
MESH = pl.DeviceIdType.MESH


def tile_of(extent, most):
    width = most
    while extent % width:
        width -= 128
    return width


def layer(
    sources, planes, cap, tn, td,
    packed, wg, wu, wd, ret,
    xbuf, gacc, uacc, hid, wbuf, dbuf, psend, precv, own, xsend, xrecv, esend,
    wsem, dsem, lsem, es, er, xs, xr, cs, cr, fs, fr, ps, pr, ys, yr, zs, zr,
):
    me = lax.axis_index("ep")
    tp = lax.axis_index("tp")
    core = lax.rem(tp, CORES)
    plane = tp // CORES
    other = plane * CORES + lax.rem(core + 1, CORES)
    teams = planes * CORES
    share = packed.shape[2]
    hidden = hid.shape[1]
    ntiles = hidden // tn
    dtiles = share // td
    total = teams * ntiles

    def peer(dx):
        return lax.rem(plane + dx, planes) * CORES + core

    def quarter(qi):
        return lax.rem(plane + planes - qi // CORES, planes) * CORES + lax.rem(core + qi % CORES, CORES)

    def weights(i, which, src):
        rows = pl.ds(pl.multiple_of(quarter(i // ntiles) * share, share), share)
        cols = pl.ds(pl.multiple_of((i % ntiles) * tn, tn), tn)
        return pltpu.make_async_copy(src.at[rows, cols], wbuf.at[i % 3, which], wsem.at[i % 3, which])

    def fetch(i):
        weights(i, 0, wg).start()
        weights(i, 1, wu).start()

    def chunk(ci):
        dx = lax.rem(ci // CORES + 1, planes)
        return lax.rem(plane + dx, planes) * CORES + lax.rem(core + 1 + ci % CORES, CORES)

    def down(i):
        cols = pl.ds(pl.multiple_of(chunk(i // dtiles) * share + (i % dtiles) * td, td), td)
        return pltpu.make_async_copy(wd.at[:, cols], dbuf.at[i % 3], dsem.at[i % 3])

    fetch(0)
    fetch(1)
    for i in range(2):
        down(i).start()

    barrier = pltpu.get_barrier_semaphore()
    for k in range(1, sources):
        pl.semaphore_signal(barrier, inc=1, device_id={"ep": lax.rem(me + k, sources), "tp": tp}, device_id_type=MESH)
    for dx in range(1, planes):
        pl.semaphore_signal(barrier, inc=1, device_id={"ep": me, "tp": peer(dx)}, device_id_type=MESH)
    pl.semaphore_signal(barrier, inc=1, device_id={"ep": me, "tp": other}, device_id_type=MESH)
    pl.semaphore_wait(barrier, sources - 1 + planes - 1 + 1)

    def rows_of(s):
        return pl.ds(pl.multiple_of(s * cap, cap), cap)

    ep_copies = [None]
    for k in range(1, sources):
        to = lax.rem(me + k, sources)
        copy = pltpu.make_async_remote_copy(
            src_ref=packed.at[to], dst_ref=xbuf.at[tp, rows_of(me)],
            send_sem=es.at[k], recv_sem=er.at[k],
            device_id={"ep": to, "tp": tp}, device_id_type=MESH)
        copy.start()
        ep_copies.append(copy)
    local = pltpu.make_async_copy(packed.at[me], xbuf.at[tp, rows_of(me)], lsem.at[0])
    local.start()
    local.wait()
    x_copies, c_copies = {}, []
    for k in range(sources):
        s = lax.rem(me - k + sources, sources)
        if k:
            ep_copies[k].wait_recv()
        for dx in range(1, planes):
            copy = pltpu.make_async_remote_copy(
                src_ref=xbuf.at[tp, rows_of(s)], dst_ref=xbuf.at[tp, rows_of(s)],
                send_sem=xs.at[dx, k], recv_sem=xr.at[dx, k],
                device_id={"ep": me, "tp": peer(dx)}, device_id_type=MESH)
            copy.start()
            x_copies[dx, k] = copy
        copy = pltpu.make_async_remote_copy(
            src_ref=xbuf.at[tp, rows_of(s)], dst_ref=xbuf.at[tp, rows_of(s)],
            send_sem=cs.at[k], recv_sem=cr.at[k],
            device_id={"ep": me, "tp": other}, device_id_type=MESH)
        copy.start()
        c_copies.append(copy)

    f_copies = {}
    for qi in range(teams):
        dx = qi // CORES
        q = quarter(qi)
        if qi == 1:
            for copy in c_copies:
                copy.wait_recv()
        elif qi > 1 and qi % CORES == 0:
            for k in range(sources):
                x_copies[dx, k].wait_recv()
            copy = pltpu.make_async_remote_copy(
                src_ref=xbuf.at[q], dst_ref=xbuf.at[q],
                send_sem=fs.at[dx], recv_sem=fr.at[dx],
                device_id={"ep": me, "tp": other}, device_id_type=MESH)
            copy.start()
            f_copies[dx] = copy
        elif qi > 1:
            f_copies[dx].wait_recv()

        def step(n, carry, qi=qi, q=q):
            i = qi * ntiles + n

            @pl.when(i + 2 < total)
            def _():
                fetch(i + 2)

            weights(i, 0, wg).wait()
            weights(i, 1, wu).wait()
            cols = pl.ds(pl.multiple_of(n * tn, tn), tn)
            gate = jnp.dot(xbuf[q], wbuf[i % 3, 0], preferred_element_type=jnp.float32)
            upper = jnp.dot(xbuf[q], wbuf[i % 3, 1], preferred_element_type=jnp.float32)
            if qi:
                gate = gate + gacc[:, cols]
                upper = upper + uacc[:, cols]
            if qi < teams - 1:
                gacc[:, cols] = gate
                uacc[:, cols] = upper
            else:
                hid[:, cols] = (gate / (1.0 + jnp.exp(-gate)) * upper).astype(jnp.bfloat16)
            return carry

        lax.fori_loop(0, ntiles, step, 0)

    dtotal = teams * dtiles
    p_copies, y_copies = {}, {}
    for ci in range(teams):
        dx = (ci // CORES + 1) % planes
        mine = ci % CORES == 1

        def dstep(n, carry, ci=ci, dx=dx, mine=mine):
            i = ci * dtiles + n

            @pl.when(i + 2 < dtotal)
            def _():
                down(i + 2).start()

            down(i).wait()
            cols = pl.ds(pl.multiple_of(n * td, td), td)
            part = jnp.dot(hid[...], dbuf[i % 3], preferred_element_type=jnp.float32)
            if mine:
                own[:, cols] = part
            else:
                psend[dx, :, cols] = part.astype(jnp.bfloat16)
            return carry

        lax.fori_loop(0, dtiles, dstep, 0)
        if not mine:
            copy = pltpu.make_async_remote_copy(
                src_ref=psend.at[dx], dst_ref=precv.at[dx],
                send_sem=ps.at[dx], recv_sem=pr.at[dx],
                device_id={"ep": me, "tp": other}, device_id_type=MESH)
            copy.start()
            p_copies[dx] = copy
        elif dx:
            p_copies[dx].wait_recv()
            for k in range(sources):
                s = lax.rem(me + k + 1, sources)
                rows = rows_of(s)
                xsend[dx - 1, rows] = (own[rows] + precv[dx, rows].astype(jnp.float32)).astype(jnp.bfloat16)
                copy = pltpu.make_async_remote_copy(
                    src_ref=xsend.at[dx - 1, rows], dst_ref=xrecv.at[dx - 1, rows],
                    send_sem=ys.at[dx, k], recv_sem=yr.at[dx, k],
                    device_id={"ep": me, "tp": peer(dx)}, device_id_type=MESH)
                copy.start()
                y_copies[dx, k] = copy
    p_copies[0].wait_recv()
    z_copies = []
    for k in range(sources):
        s = lax.rem(me + k + 1, sources)
        rows = rows_of(s)
        value = own[rows] + precv[0, rows].astype(jnp.float32)
        for dx in range(1, planes):
            y_copies[dx, k].wait_recv()
            value = value + xrecv[dx - 1, rows].astype(jnp.float32)
        if k == sources - 1:
            ret[me] = value.astype(jnp.bfloat16)
        else:
            esend[k] = value.astype(jnp.bfloat16)
            copy = pltpu.make_async_remote_copy(
                src_ref=esend.at[k], dst_ref=ret.at[me],
                send_sem=zs.at[k], recv_sem=zr.at[k],
                device_id={"ep": s, "tp": tp}, device_id_type=MESH)
            copy.start()
            z_copies.append(copy)
    for copy in z_copies:
        copy.wait_recv()
    for copy in ep_copies[1:] + list(x_copies.values()) + c_copies + list(f_copies.values()):
        copy.wait_send()
    for copy in list(p_copies.values()) + list(y_copies.values()) + z_copies:
        copy.wait_send()


def shards(tokens, expert_ids, gate_logits, w_gate, w_up, w_down):
    tok_count, width = tokens.shape
    ep_count = lax.axis_size("ep")
    tp_count = lax.axis_size("tp")
    group = ep_count // EXPERTS
    cap = tok_count // 2
    share = width // tp_count
    planes = tp_count // CORES
    hidden = w_gate.shape[2]
    first = 1.0 / (1.0 + jnp.exp(gate_logits[:, 1] - gate_logits[:, 0]))
    second = 1.0 / (1.0 + jnp.exp(gate_logits[:, 0] - gate_logits[:, 1]))
    experts = jnp.arange(EXPERTS, dtype=jnp.int32)[None, :]
    hit0 = expert_ids[:, 0:1] == experts
    hit1 = expert_ids[:, 1:2] == experts
    row = lax.broadcasted_iota(jnp.int32, (tok_count, tok_count), 0)
    col = lax.broadcasted_iota(jnp.int32, (tok_count, tok_count), 1)
    earlier = jnp.dot(
        (col < row).astype(jnp.bfloat16), (hit0 | hit1).astype(jnp.bfloat16),
        preferred_element_type=jnp.float32).astype(jnp.int32)
    dest0 = jnp.sum(jnp.where(hit0, earlier + experts * cap, 0), axis=1)
    dest1 = jnp.sum(jnp.where(hit1, earlier + experts * cap, 0), axis=1)
    places = jnp.arange(EXPERTS * cap, dtype=jnp.int32)
    pick = ((places[:, None] == dest0[None, :]) | (places[:, None] == dest1[None, :])).astype(jnp.bfloat16)
    quarter = lax.dynamic_slice_in_dim(tokens, lax.axis_index("tp") * share, share, 1)
    packed = jnp.dot(pick, quarter, preferred_element_type=jnp.float32).astype(jnp.bfloat16)
    packed = jnp.repeat(packed.reshape(EXPERTS, cap, share), group, axis=0)

    tn = tile_of(hidden, 512)
    td = tile_of(share, 256)
    rows = ep_count * cap
    vmem = pl.BlockSpec(memory_space=pltpu.VMEM)
    hbm = pl.BlockSpec(memory_space=pl.ANY)
    dma = pltpu.SemaphoreType.DMA
    bf16, f32 = jnp.bfloat16, jnp.float32
    ret = pl.pallas_call(
        functools.partial(layer, ep_count, planes, cap, tn, td),
        out_shape=jax.ShapeDtypeStruct((ep_count, cap, share), bf16),
        in_specs=[vmem, hbm, hbm, hbm],
        out_specs=vmem,
        scratch_shapes=[
            pltpu.VMEM((tp_count, rows, share), bf16),
            pltpu.VMEM((rows, hidden), f32),
            pltpu.VMEM((rows, hidden), f32),
            pltpu.VMEM((rows, hidden), bf16),
            pltpu.VMEM((3, 2, share, tn), bf16),
            pltpu.VMEM((3, hidden, td), bf16),
            pltpu.VMEM((planes, rows, share), bf16),
            pltpu.VMEM((planes, rows, share), bf16),
            pltpu.VMEM((rows, share), f32),
            pltpu.VMEM((planes - 1, rows, share), bf16),
            pltpu.VMEM((planes - 1, rows, share), bf16),
            pltpu.VMEM((ep_count, cap, share), bf16),
            dma((3, 2)),
            dma((3,)),
            dma((1,)),
            dma((ep_count,)), dma((ep_count,)),
            dma((planes, ep_count)), dma((planes, ep_count)),
            dma((ep_count,)), dma((ep_count,)),
            dma((planes,)), dma((planes,)),
            dma((planes,)), dma((planes,)),
            dma((planes, ep_count)), dma((planes, ep_count)),
            dma((ep_count,)), dma((ep_count,)),
        ],
        compiler_params=pltpu.CompilerParams(
            collective_id=0, has_side_effects=True, vmem_limit_bytes=60 * 1024 * 1024),
        name="expert_layer",
    )(packed, w_gate[0], w_up[0], w_down[0])

    results = ret.reshape(EXPERTS * group * cap, share)
    home = jnp.arange(EXPERTS * group * cap, dtype=jnp.int32)[None, :]
    slot_at = (home // (group * cap)) * cap + home % cap
    out0 = jnp.dot((slot_at == dest0[:, None]).astype(bf16), results, preferred_element_type=f32)
    out1 = jnp.dot((slot_at == dest1[:, None]).astype(bf16), results, preferred_element_type=f32)
    return (first[:, None] * out0 + second[:, None] * out1).astype(bf16)


def solution(mesh):
    placed = (
        P("ep", None),
        P("ep", None),
        P("ep", None),
        P("ep", None, "tp"),
        P("ep", None, "tp"),
        P("ep", "tp", None),
    )
    return jax.shard_map(
        shards, mesh=mesh, in_specs=placed, out_specs=P("ep", "tp"), check_vma=False
    )
```

time: 242 us -> 115 us (0.48); the launches traced: 238 us -> 115 us
  Pallas kernels: 0 us -> 109 us
  waiting for transfers between devices: 103 us -> 0 us
  matrix products: 71.6 us -> 5.4 us
  blocking collectives: 29.3 us -> 0 us
  between operations: 13.5 us -> 0.04 us
  local copies, waits for them, and re-layouts: 9.46 us -> 1.13 us
  starting transfers between devices: 6.22 us -> 0 us
  other arithmetic: 5.2 us -> 0.02 us
    pallas_call x0 -> x1, Pallas kernels: none -> 109 us  [shards(): pl.pallas_call(functools.partial(layer, ep_count, planes, cap, tn, td), o...]
    dot_general x3 -> x4, matrix products: 71.6 us -> 5.4 us  [the longest x1 2.28 us: shards(): jnp.dot((slot_at == dest1[:, None]).astype(bf16), results, preferred_elem...]
    reduce_scatter x1 -> x0, waiting for transfers between devices: 44.6 us -> none  [shards(): lax.psum_scatter(lax.dot_general(wpiece, hidden, (((0,), (1,)), ((), ()))...]
    all_gather x1 -> x0, waiting for transfers between devices: 35.3 us -> none  [shards(): received = lax.all_gather(received, 'tp', axis=2, tiled=True)]
    all_to_all x1 -> x0, blocking collectives: 29.3 us -> none  [shards(): lax.all_to_all(outgoing, 'ep', split_axis=0, concat_axis=0, tiled=True)]
    all_to_all x1 -> x0, waiting for transfers between devices: 22.8 us -> none  [shards(): lax.all_to_all(shares.astype(jnp.bfloat16), 'ep', split_axis=1, concat_ax...]
    all_to_all x1 -> x0, starting transfers between devices: 6 us -> none  [shards(): lax.all_to_all(shares.astype(jnp.bfloat16), 'ep', split_axis=1, concat_ax...]
    gather x3 -> x0, local copies, waits for them, and re-layouts: 5.94 us -> none  [the longest x2 3.88 us: shards(): jnp.take(results, columns.reshape(-1), axis=1)]
  transfers between devices with their start and end apart: 3 -> 0, of which waited for: 3 -> 0; matrix products, arithmetic and copies ran while one was open for 0% -> 0% of each run, Pallas kernels for 0% -> 0%
where the time goes in v1:
time: 115 us
  Pallas kernels  109 us (95%)
  matrix products  5.4 us (5%)
    pallas_call x1, Pallas kernels, shards(): pl.pallas_call(functools.partial(layer, ep_count, planes, cap, tn, td), o...  109 us

profile of v1, /device:TPU:28, one launch (start us, length us, event | category | flops | bytes accessed | tf_op | source)
XLA Modules:
  0.0 115.3 jit_solution(4187337094887945462)
XLA Ops:
  0.0 0.0 copy-start
  0.0 0.8 slice_bitcast_fusion.1
  0.8 0.1 select_reduce_fusion.1
  0.9 0.3 copy-done
  1.3 1.4 %convolution_convert_fusion = bf16[512,1024]{1,0:T(8,128)(2,1)} fusion(bf16[128,4096]{1,0:T(8,128)(2,1)S(1)} %copy-done, s32[]{:T(128)S(6)} %select_n.40, s32[128]{0:T(128)S(1)} %get-tuple-element.6, s32[128]{0:T(128)S(1)} %get-tuple-element.5), kind=kOutput, calls=%fused_computation | convolution fusion | flops 134938624 | bytes 1311748 | tf_op jit(solution)/shard_map/dot_general | solution.py:247
  2.7 0.0 copy-start.1
  2.7 108.7 %expert_layer.1 = bf16[8,64,1024]{2,1,0:T(8,128)(2,1)} custom-call(bf16[8,64,1024]{2,1,0:T(8,128)(2,1)} %bitcast.20, bf16[4096,3584]{1,0:T(8,128)(2,1)} %bitcast.15, bf16[4096,3584]{1,0:T(8,128)(2,1)} %bitcast.16, bf16[3584,4096]{1,0:T(8,128)(2,1)} %bitcast.17), custom_call_target="tpu_custom_call" | custom-call | tf_op jit(solution)/shard_map/expert_layer/pallas_call | solution.py:257
  111.4 0.0 copy-done.1
  111.4 1.6 %convolution_multiply_fusion.1 = f32[128,1024]{1,0:T(8,128)S(1)} fusion(bf16[512,1024]{1,0:T(8,128)(2,1)} %bitcast.18, f32[128]{0:T(128)S(1)} %get-tuple-element.8, s32[512]{0:T(512)S(1)} %fusion.21, s32[128]{0:T(128)S(1)} %get-tuple-element.5), kind=kOutput, calls=%fused_computation.3 | convolution fusion | flops 134414336 | bytes 1575936 | tf_op jit(solution)/shard_map/dot_general | solution.py:294
  113.0 2.3 %fusion.1 = bf16[128,1024]{1,0:T(8,128)(2,1)} fusion(f32[128,1024]{1,0:T(8,128)S(1)} %convolution_multiply_fusion.1, bf16[512,1024]{1,0:T(8,128)(2,1)} %bitcast.19, f32[128]{0:T(128)S(1)} %get-tuple-element.7, s32[512]{0:T(512)S(1)} %fusion.21, s32[128]{0:T(128)S(1)} %get-tuple-element.6), kind=kOutput, calls=%fused_computation.4 | convolution fusion | flops 134676480 | bytes 1838080 | tf_op jit(solution)/shard_map/dot_general | solution.py:295
  (3 shorter events, 0.0 us)
Async XLA Ops:
  0.0 1.3 %copy-start = (bf16[128,4096]{1,0:T(8,128)(2,1)S(1)}, bf16[128,4096]{1,0:T(8,128)(2,1)}, u32[]{:S(2)}) copy-start(bf16[128,4096]{1,0:T(8,128)(2,1)} %param.6) | copy-start | bytes 3145732
  2.7 108.7 %copy-start.1 = (f32[128,2]{0,1:T(2,128)S(1)}, f32[128,2]{0,1:T(2,128)}, u32[]{:S(2)}) copy-start(f32[128,2]{0,1:T(2,128)} %param.8) | copy-start | bytes 3076
